TPU v7x, 32 devices: a whole 2x2x4 slice. The times are simulated.
32 devices in a mesh: section: 2 (over y), freq: 16 (over z, x, core).
Axes of the slice: x: 2, y: 2, z: 4, core: 2. Of those that a mesh axis runs over, the one named last changes fastest.
Arguments:
- spectra: float32 [4, 16, 131072], P('section', None, 'freq'), may hold values from 0.1 to 90, as said below
- channel_gain: float32 [131072], P('freq'), may hold values from 0.5 to 2
- bandpass_bin: int32 [131072], P('freq'), may hold values from 0 to 63, never falling along the last dimension, each value on 1 to 8192 neighbouring positions
- drift_range: int32 [4], replicated, may hold values from 1 to 2, as said below
- hit_cutoff: int32 [4, 2, 16], replicated, may hold values from 0 to 1023
Outputs:
- drift_score: float32 [4, 2, 131072], P(None, 'section', 'freq')
Inputs may be any that keep to these rules, and one draw needn't show every extreme that they name: `spectra`: every entry is positive. `bandpass_bin`: the bins never fall along the channels and each of the 64 bins holds 1 to 8192 channels. `drift_range`: some group reaches 2 and some other group searches stride 1 only.
All inputs are finite; a program needn't handle non-finite values.
Results may differ from a plain program's by a relative error of at most 0.0003.
Values sent between devices are 32-bit elements; how exact they have to be, the bound alone decides.
No kernel may reach another device: no remote copies, remote signals or barrier semaphores. Data moves between devices by JAX's collectives and lax.ppermute only.
A program may use at most 64 MiB of HBM per device.

v0:
```python
import dataclasses
import functools

import jax
import jax.numpy as jnp
from jax import lax
from jax.experimental import pallas as pl
from jax.experimental.pallas import tpu as pltpu
from jax.sharding import PartitionSpec as P


LANES = 128
SUBS = 8
BOTH = ("section", "freq")
CHUNK = 8
NEVER = 3e38
VMEM = pl.BlockSpec(memory_space=pltpu.VMEM)
SMEM = pl.BlockSpec(memory_space=pltpu.SMEM)
HBM = pl.BlockSpec(memory_space=pltpu.HBM)
PARAMS = pltpu.CompilerParams(vmem_limit_bytes=16 * 2**20)


@dataclasses.dataclass(frozen=True)
class Sizes:
    groups: int
    integrations: int
    bin_tiles: int
    margin: int
    rates: int
    strides: int

    @property
    def extra(self):
        return -(-self.margin // SUBS) * SUBS + SUBS

    @property
    def head(self):
        return LANES - -(-self.margin // SUBS) * SUBS

    @property
    def main_span(self):
        return LANES + SUBS

    @property
    def tail_span(self):
        return LANES - self.head + self.extra


def lane_iota():
    return lax.broadcasted_iota(jnp.int32, (SUBS, LANES), 1)


def row_iota():
    return lax.broadcasted_iota(jnp.int32, (SUBS, LANES), 0)


def spectra_rows(x_ref, group, t, first, rows, cols, integrations):
    block = group * (integrations // SUBS) + t // SUBS
    return x_ref[pl.ds((block * cols + first) * SUBS + t % SUBS, rows, stride=SUBS), :]


def pack_count(margin):
    room = 1 << (margin - 1).bit_length()
    return LANES // room, room


def bin_kernel(
    groups,
    integrations,
    bin_tiles,
    margin,
    x_hbm,
    gain_hbm,
    bins_hbm,
    packed_ref,
    x_ref,
    gain_ref,
    bins_ref,
    sems,
):
    cols = gain_ref.shape[0]
    tiles = cols // SUBS
    group_rows = integrations * cols
    copies = [
        pltpu.make_async_copy(bins_hbm, bins_ref, sems.at[0]),
        pltpu.make_async_copy(gain_hbm, gain_ref, sems.at[1]),
    ]
    for group in range(groups):
        part = pl.ds(group * group_rows, group_rows)
        copies.append(pltpu.make_async_copy(x_hbm.at[part], x_ref.at[part], sems.at[2 + group]))
    for copy in copies:
        copy.start()
    lane, row = lane_iota(), row_iota()
    copies[0].wait()
    bins = [bins_ref[tile * SUBS : (tile + 1) * SUBS, :] for tile in range(tiles)]
    first, last = jnp.min(bins[0]), jnp.max(bins[-1])
    copies[1].wait()
    summed, rims = [], []
    for group in range(groups):
        copies[2 + group].wait()
        for block in range(integrations // SUBS):
            at = (group * (integrations // SUBS) + block) * cols * SUBS
            rims.append(x_ref[at : at + SUBS, :] * gain_ref[0:1, :])
        for tile in range(tiles):
            parts = [
                spectra_rows(x_ref, group, t, tile * SUBS, SUBS, cols, integrations)
                for t in range(integrations)
            ]
            while len(parts) > 1:
                parts = [a + b for a, b in zip(parts[0::2], parts[1::2])]
            summed.append(parts[0] * gain_ref[tile * SUBS : (tile + 1) * SUBS, :])
    side, room = pack_count(margin)
    for at in range(0, len(rims), side):
        packed = rims[at]
        for place, rim in enumerate(rims[at + 1 : at + side], 1):
            packed = jnp.where(lane // room == place, pltpu.roll(rim, place * room, 1), packed)
        to = 2 * bin_tiles * SUBS + at // side * SUBS
        packed_ref[to : to + SUBS, :] = packed

    def some_bins(step, tables):
        for u in range(CHUNK):
            b = first + step * CHUNK + u
            masks = [part == b for part in bins]
            stacked = jnp.zeros((SUBS, LANES), jnp.float32)
            for quantity in range(groups + 1):
                partial = jnp.zeros((SUBS, LANES), jnp.float32)
                for tile in range(tiles):
                    value = 1.0 if quantity == groups else summed[quantity * tiles + tile]
                    partial = partial + jnp.where(masks[tile], value, 0.0)
                stacked = jnp.where(row == quantity, jnp.sum(partial, axis=0, keepdims=True), stacked)
            total = jnp.sum(stacked, axis=1, keepdims=True)
            tables = tuple(
                table + jnp.where(lane == b - q * LANES, total, 0.0) for q, table in enumerate(tables)
            )
        return tables

    start = tuple(jnp.zeros((SUBS, LANES), jnp.float32) for _ in range(bin_tiles))
    tables = lax.fori_loop(0, (last - first) // CHUNK + 1, some_bins, start)
    rim_bins = jnp.broadcast_to(bins_ref[0:1, :].astype(jnp.float32), (SUBS, LANES))
    rim_bins_row = SUBS - 2 + lax.rem(lax.axis_index("freq"), 2)
    for q, table in enumerate(tables):
        shifted = pltpu.roll(table, groups + 1, 0)
        packed_ref[(bin_tiles + q) * SUBS : (bin_tiles + q + 1) * SUBS, :] = jnp.where(
            (row > groups) & (row <= 2 * groups), shifted, 0.0
        )
        if q == 0:
            table = jnp.where(row == rim_bins_row, rim_bins, table)
        packed_ref[q * SUBS : (q + 1) * SUBS, :] = table


def turn_kernel(groups, integrations, x_ref, cut_hbm, reach_hbm, turned_ref, cuts_ref, cut_ref, reach_ref, sems):
    copies = [
        pltpu.make_async_copy(cut_hbm, cut_ref, sems.at[0]),
        pltpu.make_async_copy(reach_hbm, reach_ref, sems.at[1]),
    ]
    for copy in copies:
        copy.start()
    cols = LANES // groups
    for t in range(integrations):
        block = jnp.concatenate(
            [spectra_rows(x_ref, group, t, 0, cols, cols, integrations) for group in range(groups)], axis=0
        )
        turned_ref[t * LANES : (t + 1) * LANES, :] = block.T
    for copy in copies:
        copy.wait()
    lane = lax.broadcasted_iota(jnp.int32, (1, LANES), 1)
    section = lax.axis_index("section")
    for index in range(cut_ref.shape[1]):
        for drift in range(integrations):
            line = jnp.zeros((1, LANES), jnp.float32)
            for group in range(groups):
                group_id = section * groups + group
                cut = cut_ref[group_id, index, drift].astype(jnp.float32) * (4.0 / 256.0)
                cut = jnp.where(index + 1 <= reach_ref[group_id], cut, NEVER)
                line = jnp.where(lane // cols == group, cut, line)
            at = index * integrations + drift
            cuts_ref[at : at + 1, :] = line


def look_up(rows, bins):
    found = None
    for q, values in enumerate(rows):
        spread = jnp.broadcast_to(values, bins.shape)
        index = bins if len(rows) == 1 else jnp.clip(bins - q * LANES, 0, LANES - 1)
        value = jnp.take_along_axis(spread, index, axis=1)
        found = value if q == 0 else jnp.where(bins >= q * LANES, value, found)
    return found


def inverse_levels(groups, integrations, bin_tiles, table_ref):
    first = lax.axis_index("section") * groups
    result = [[] for _ in range(groups)]
    for q in range(bin_tiles):
        rows = [table_ref[q * SUBS + r : q * SUBS + r + 1, :] for r in range(2 * groups + 1)]
        running = sum(rows[groups + 2 :], rows[groups + 1])
        for group in range(groups):
            running = running + rows[group]
            tally = rows[groups] * ((first + group + 1) * integrations).astype(jnp.float32)
            result[group].append(tally / running)
    return result


def main_kernel(
    sizes,
    gain_ref,
    bins_ref,
    own_ref,
    rim_bins_ref,
    rim_ref,
    turned_ref,
    cuts_ref,
    normal_ref,
    tail_ref,
    rim_index_ref,
    head_ref,
    *later_refs,
):
    groups, integrations = sizes.groups, sizes.integrations
    tiles = gain_ref.shape[0] // SUBS
    inverse = inverse_levels(groups, integrations, sizes.bin_tiles, own_ref)
    factors = []
    for group in range(groups):
        for tile in range(tiles):
            part = slice(tile * SUBS, (tile + 1) * SUBS)
            factors.append(look_up(inverse[group], bins_ref[part, :]) * gain_ref[part, :])
    factor = jnp.concatenate(factors, axis=0).T
    cols = LANES // groups
    side, room = pack_count(sizes.margin)
    rims = []
    for group in range(groups):
        for block in range(integrations // SUBS):
            at = group * (integrations // SUBS) + block
            rim = rim_ref[at // side * SUBS : (at // side + 1) * SUBS, :]
            rims.append(pltpu.roll(rim, LANES - at % side * room, 1) if at % side else rim)
        rims.append(jnp.zeros((cols - integrations, LANES), jnp.float32))
    raw = jnp.concatenate(rims, axis=0).T[: sizes.extra]
    rim_index = jnp.broadcast_to(rim_bins_ref[0:1, :], (LANES, LANES)).T
    rim_index_ref[...] = rim_index[: sizes.extra].astype(jnp.int32)
    last_col = lax.broadcasted_iota(jnp.int32, (sizes.extra, LANES), 1) % cols == cols - 1
    for t in range(integrations):
        normal = turned_ref[t * LANES : (t + 1) * LANES, :] * factor - 1.0
        at = t * sizes.main_span
        normal_ref[at : at + LANES, :] = normal
        normal_ref[at + LANES : at + sizes.main_span, :] = jnp.zeros((sizes.main_span - LANES, LANES), jnp.float32)
        at = t * sizes.tail_span
        tail_ref[at : at + LANES - sizes.head, :] = normal[sizes.head :]
        outer = pltpu.roll(raw, cols - 1 - t, 1) if cols - 1 - t else raw
        tail_ref[at + LANES - sizes.head : at + sizes.tail_span, :] = jnp.where(
            last_col, outer, pltpu.roll(normal[: sizes.extra], LANES - 1, 1)
        )
    for index in range(sizes.strides):
        scores = tree(sizes, 1, index, normal_ref, sizes.main_span, sizes.head, cuts_ref, later_refs)
        head_ref[index * sizes.head : (index + 1) * sizes.head, :] = scores


def rim_kernel(
    sizes, next_ref, rim_index_ref, half_tail_ref, head_ref, cuts_ref, tail_ref, out_ref, *later_refs
):
    groups, integrations = sizes.groups, sizes.integrations
    cols = LANES // groups
    lane = lane_iota()
    at_end = lax.axis_index("freq") == lax.axis_size("freq") - 1
    last_col = lane % cols == cols - 1
    inverse = inverse_levels(groups, integrations, sizes.bin_tiles, next_ref)
    inner = LANES - sizes.head
    for row in range(0, sizes.extra, SUBS):
        index = rim_index_ref[row : row + SUBS, :]
        level = look_up(inverse[0], index)
        for group in range(1, groups):
            level = jnp.where(lane // cols == group, look_up(inverse[group], index), level)
        for t in range(integrations):
            at = t * sizes.tail_span + inner + row
            half = half_tail_ref[at : at + SUBS, :]
            edge = jnp.where(at_end, 0.0, half * level - 1.0)
            tail_ref[at : at + SUBS, :] = jnp.where(last_col, edge, half)
    for t in range(integrations):
        at = t * sizes.tail_span
        tail_ref[at : at + inner, :] = half_tail_ref[at : at + inner, :]
    for index in range(sizes.strides):
        head = head_ref[index * sizes.head : (index + 1) * sizes.head, :]
        rest = tree(sizes, 1, index, tail_ref, sizes.tail_span, LANES - sizes.head, cuts_ref, later_refs)
        put_scores(sizes, out_ref, index, [head, rest])


def tree_kernel(sizes, hop, normal_ref, tail_ref, cuts_ref, out_ref, *later_refs):
    half = len(later_refs) // 2
    for index in range(sizes.strides):
        head = tree(sizes, hop, index, normal_ref, sizes.main_span, sizes.head, cuts_ref, later_refs[:half])
        rest = tree(
            sizes, hop, index, tail_ref, sizes.tail_span, LANES - sizes.head, cuts_ref, later_refs[half:]
        )
        put_scores(sizes, out_ref, index, [head, rest])


def own_kernel(sizes, normal_ref, tail_ref, cuts_ref, out_hbm, scores_ref, sem, *later_refs):
    tree_kernel(sizes, 0, normal_ref, tail_ref, cuts_ref, scores_ref, *later_refs)
    rows = scores_ref.shape[0]
    at = pl.multiple_of(lax.axis_index("section") * rows, SUBS)
    copy = pltpu.make_async_copy(scores_ref, out_hbm.at[pl.ds(at, rows)], sem)
    copy.start()
    copy.wait()


def place_kernel(hop, scores_ref, _, out_hbm, sem):
    rows, sections = scores_ref.shape[0], lax.axis_size("section")
    at = pl.multiple_of(lax.rem(lax.axis_index("section") + sections - hop, sections) * rows, SUBS)
    copy = pltpu.make_async_copy(scores_ref, out_hbm.at[pl.ds(at, rows)], sem)
    copy.start()
    copy.wait()


def put_scores(sizes, out_ref, index, parts):
    scores = jnp.concatenate(parts, axis=0).T
    cols = LANES // sizes.groups
    for group in range(sizes.groups):
        at = (group * sizes.strides + index) * cols
        out_ref[at : at + cols, :] = scores[group * cols : (group + 1) * cols]


def tree(sizes, hop, index, normal_ref, span, length, cuts_ref, later_refs):
    integrations = sizes.integrations
    levels = integrations.bit_length() - 1
    target = lax.rem(lax.axis_index("section") + hop, lax.axis_size("section"))
    stride = target * sizes.strides + index + 1

    def values(level, block, at):
        if level == 0:
            return [normal_ref[block * span + at : block * span + at + SUBS, :]]
        former = values(level - 1, 2 * block, at)
        rows = 2 ** (level - 1)
        result = []
        for half, anchor in enumerate(former):
            if level == 1:
                ref, base = normal_ref, (2 * block + 1) * span
            else:
                ref, base = later_refs[level - 2], (block * rows + half) * span
            for steps in (half, half + 1):
                result.append(anchor + ref[pl.ds(base + at + steps * stride, SUBS), :])
        return result

    for level in range(1, levels):
        reach = min(span, length + -(-(integrations - 2**level) * sizes.rates // SUBS) * SUBS)
        reach = min(reach, span - SUBS)
        for block in range(1, integrations >> level, 2):
            for at in range(0, reach, SUBS):
                for drift, value in enumerate(values(level, block, at)):
                    row = ((block // 2) * 2**level + drift) * span + at
                    later_refs[level - 1][row : row + SUBS, :] = value
    parts = []
    for at in range(0, length, SUBS):
        score = jnp.zeros((SUBS, LANES), jnp.float32)
        for drift, value in enumerate(values(levels, 0, at)):
            cut = cuts_ref[pl.ds((stride - 1) * integrations + drift, 1), :]
            score = score + jnp.maximum(value - cut, 0.0)
        parts.append(score * (0.25 / integrations))
    return jnp.concatenate(parts, axis=0)


def far(value):
    return pltpu.with_memory_space_constraint(value, pltpu.HBM)


def swap(value, partner):
    sections, freqs = lax.axis_size("section"), lax.axis_size("freq")
    route = []
    for section in range(sections):
        for freq in range(freqs):
            to_section, to_freq = partner(section, freq)
            route.append((section * freqs + freq, to_section * freqs + to_freq))
    return lax.ppermute(value, BOTH, route)


def search(spectra, channel_gain, bandpass_bin, drift_range, hit_cutoff):
    groups, integrations, chan_dev = spectra.shape
    sections, freqs = lax.axis_size("section"), lax.axis_size("freq")
    section, freq = lax.axis_index("section"), lax.axis_index("freq")
    total_bins = 4 * freqs
    bin_tiles = -(-total_bins // LANES)
    rates = hit_cutoff.shape[1]
    strides = rates // sections
    margin = rates * (integrations - 1)
    cols = chan_dev // LANES
    sizes = Sizes(groups, integrations, bin_tiles, margin, rates, strides)
    blocks = integrations // SUBS
    assert cols % SUBS == 0 and integrations % SUBS == 0 and margin <= LANES - SUBS
    assert sections > 1 and groups * cols == LANES and integrations <= cols
    assert freqs % 2 == 0 and 2 * groups + 1 <= SUBS - 2 and rates % sections == 0
    x = spectra.reshape(groups, blocks, SUBS, cols, LANES).transpose(0, 1, 3, 2, 4)
    x = x.reshape(groups * blocks * cols * SUBS, LANES)
    gain = channel_gain.reshape(cols, LANES)
    bins = bandpass_bin.reshape(cols, LANES)
    shape = functools.partial(jax.ShapeDtypeStruct, dtype=jnp.float32)
    side, _ = pack_count(margin)
    rim_tiles = -(-groups * blocks // side)

    packed, x_near, gain_near, bins_near = pl.pallas_call(
        functools.partial(bin_kernel, groups, integrations, bin_tiles, margin),
        out_shape=(
            shape(((2 * bin_tiles + rim_tiles) * SUBS, LANES)),
            shape(x.shape),
            shape(gain.shape),
            jax.ShapeDtypeStruct(bins.shape, bins.dtype),
        ),
        in_specs=[HBM] * 3,
        out_specs=(VMEM,) * 4,
        scratch_shapes=[pltpu.SemaphoreType.DMA((2 + groups,))],
        compiler_params=PARAMS,
        name="bin_sums",
    )(far(x), far(gain), far(bins))

    turned, cuts = pl.pallas_call(
        functools.partial(turn_kernel, groups, integrations),
        out_shape=(shape((integrations * LANES, LANES)), shape((rates * integrations, LANES))),
        in_specs=[VMEM, HBM, HBM],
        out_specs=(VMEM, VMEM),
        scratch_shapes=[
            pltpu.SMEM(hit_cutoff.shape, jnp.int32),
            pltpu.SMEM(drift_range.shape, jnp.int32),
            pltpu.SemaphoreType.DMA((2,)),
        ],
        compiler_params=PARAMS,
        cost_estimate=pl.CostEstimate(flops=10**7, bytes_accessed=0, transcendentals=0),
        name="turn",
    )(x_near, far(hit_cutoff), far(drift_range))

    mate = lambda s, f: (s, f ^ 1)

    def across(s, f):
        other = f + 1 if f % 2 else f - 1
        if 0 <= other < freqs:
            return (s, other)
        return (s ^ 1, f) if sections % 2 == 0 else (s, f)

    rows = bin_tiles * SUBS
    from_mate = swap(packed, mate)
    pairs = packed[: 2 * rows] + from_mate[: 2 * rows]
    pair, shifted_pair = pairs[:rows], pairs[rows:]
    to_across = jnp.concatenate([pair, packed[2 * rows :]], axis=0)
    to_across, shifted_pair = lax.optimization_barrier((to_across, shifted_pair))
    from_across = swap(to_across, across)
    has_across = jnp.logical_and(freq != 0, freq != freqs - 1)
    own = pair + jnp.where(has_across, from_across[:rows], 0.0)
    if sections == 2:

        def across_other(s, f):
            return (1, across(s, f)[1]) if s == 0 else (0, f ^ 1)

        beside = swap(shifted_pair, lambda s, f: (1 - s, f))
        beside_across = swap(shifted_pair, across_other)
        earlier = beside + jnp.where(has_across, beside_across, 0.0)
        own = own + jnp.where(section == 1, earlier, 0.0)
    else:
        all_shifted = lax.all_gather(shifted_pair, "section")
        is_earlier = lax.broadcasted_iota(jnp.int32, (sections, 1, 1), 0) < section
        earlier = jnp.sum(jnp.where(is_earlier, all_shifted, 0.0), axis=0)
        earlier_across = swap(earlier, across)
        own = own + earlier + jnp.where(has_across, earlier_across, 0.0)
    odd = freq % 2 == 1
    following = jnp.where(odd, own, swap(own, mate))
    next_rim = jnp.where(odd, from_across[rows:], from_mate[2 * rows :])
    next_bins = jnp.where(odd, from_across[SUBS - 2 : SUBS - 1], from_mate[SUBS - 1 : SUBS])

    def work(flops):
        return pl.CostEstimate(flops=flops, bytes_accessed=0, transcendentals=0)

    def later(span):
        half = pltpu.VMEM((integrations // 2 * span, LANES), jnp.float32)
        return [half] * (integrations.bit_length() - 2)

    normal, half_tail, rim_index, head = pl.pallas_call(
        functools.partial(main_kernel, sizes),
        out_shape=(
            shape((integrations * sizes.main_span, LANES)),
            shape((integrations * sizes.tail_span, LANES)),
            jax.ShapeDtypeStruct((sizes.extra, LANES), jnp.int32),
            shape((strides * sizes.head, LANES)),
        ),
        in_specs=[VMEM] * 7,
        out_specs=(VMEM,) * 4,
        scratch_shapes=later(sizes.main_span),
        compiler_params=PARAMS,
        cost_estimate=work(10**7),
        name="main",
    )(gain_near, bins_near, own, next_bins, next_rim, turned, cuts)
    scores_shape = shape((groups * strides * cols, LANES))
    tail, first_scores = pl.pallas_call(
        functools.partial(rim_kernel, sizes),
        out_shape=(shape(half_tail.shape), scores_shape),
        in_specs=[VMEM] * 5,
        out_specs=(VMEM, VMEM),
        scratch_shapes=later(sizes.tail_span),
        compiler_params=PARAMS,
        name="rim",
    )(following, rim_index, half_tail, head, cuts)

    def scores(hop):
        return pl.pallas_call(
            functools.partial(tree_kernel, sizes, hop),
            out_shape=scores_shape,
            in_specs=[VMEM] * 3,
            out_specs=VMEM,
            scratch_shapes=later(sizes.main_span) + later(sizes.tail_span),
            compiler_params=PARAMS,
            cost_estimate=work(10**7),
            name="tree",
        )(normal, tail, cuts)

    arrived = []
    for hop in range(1, sections):
        sent = first_scores if hop == 1 else scores(hop)
        arrived.append(swap(sent, lambda s, f: ((s + hop) % sections, f)))
    out_shape = shape((sections * groups * strides * cols, LANES))
    out = pl.pallas_call(
        functools.partial(own_kernel, sizes),
        out_shape=out_shape,
        in_specs=[VMEM] * 3,
        out_specs=HBM,
        scratch_shapes=[pltpu.VMEM(scores_shape.shape, jnp.float32), pltpu.SemaphoreType.DMA]
        + later(sizes.main_span)
        + later(sizes.tail_span),
        compiler_params=PARAMS,
        cost_estimate=work(10**7),
        name="own",
    )(normal, tail, cuts)
    for hop, part in enumerate(arrived, 1):
        out = pl.pallas_call(
            functools.partial(place_kernel, hop),
            out_shape=out_shape,
            in_specs=[VMEM, HBM],
            out_specs=HBM,
            scratch_shapes=[pltpu.SemaphoreType.DMA],
            input_output_aliases={1: 0},
            compiler_params=PARAMS,
            name="place",
        )(part, far(out))
    return out.reshape(sections * groups, strides, chan_dev)


def solution(mesh):
    return jax.shard_map(
        search,
        mesh=mesh,
        in_specs=(P("section", None, "freq"), P("freq"), P("freq"), P(), P()),
        out_specs=P(None, "section", "freq"),
        check_vma=False,
    )
```

profile of v0, /device:TPU:0, one launch (start us, length us, event | category | flops | bytes accessed | tf_op | source)
XLA Modules:
  0.0 16.5 jit_solution(1879691778108523408)
XLA Ops:
  0.0 1.5 %bin_sums.1 = (f32[24,128]{1,0:T(8,128)S(1)}, f32[2048,128]{1,0:T(8,128)S(1)}, f32[64,128]{1,0:T(8,128)S(1)}, s32[64,128]{1,0:T(8,128)S(1)}) custom-call(f32[2048,128]{1,0:T(8,128)} %bitcast.8, f32[64,128]{1,0:T(8,128)} %bitcast.9, s32[64,128]{1,0:T(8,128)} %bitcast.10), custom_call_target="tpu_custom_call" | custom-call | tf_op jit(solution)/shard_map/bin_sums/pallas_call | solution.py:396
  1.5 0.6 %collective-permute-start = (f32[24,128]{1,0:T(8,128)S(1)}, f32[24,128]{1,0:T(8,128)S(1)}, u32[]{:S(2)}, u32[]{:S(2)}) collective-permute-start(f32[24,128]{1,0:T(8,128)S(1)} %get-tuple-element.19), channel_id=1, source_target_pairs={{0,1},{1,0},{2,3},{3,2},{4,5},{5,4},{6,7},{7,6},{8,9},{9,8},{10,11... | collective-permute-start | bytes 36872 | tf_op jit(solution)/shard_map/ppermute | solution.py:370
  2.1 0.8 %collective-permute-done = f32[24,128]{1,0:T(8,128)S(1)} collective-permute-done((f32[24,128]{1,0:T(8,128)S(1)}, f32[24,128]{1,0:T(8,128)S(1)}, u32[]{:S(2)}, u32[]{:S(2)}) %collective-permute-start) | collective-permute-done | bytes 12320 | tf_op jit(solution)/shard_map/ppermute | solution.py:370
  2.9 2.9 %collective-permute-start.1 = (f32[16,128]{1,0:T(8,128)S(1)}, f32[16,128]{1,0:T(8,128)S(1)}, u32[]{:S(2)}, u32[]{:S(2)}) collective-permute-start(f32[16,128]{1,0:T(8,128)S(1)} %pad_maximum_fusion), channel_id=1, source_target_pairs={{0,16},{1,2},{2,1},{3,4},{4,3},{5,6},{6,5},{7,8},{8,7},{9,10},{10,... | collective-permute-start | bytes 24584 | tf_op jit(solution)/shard_map/ppermute | solution.py:370
  5.8 0.1 collective-permute-start.2
  5.9 1.9 %collective-permute-start.3 = (f32[8,128]{1,0:T(8,128)S(1)}, f32[8,128]{1,0:T(8,128)S(1)}, u32[]{:S(2)}, u32[]{:S(2)}) collective-permute-start(f32[8,128]{1,0:T(8,128)S(1)} %get-tuple-element.21), channel_id=1, source_target_pairs={{0,16},{1,18},{2,17},{3,20},{4,19},{5,22},{6,21},{7,24},{8,23},{9,... | collective-permute-start | bytes 12296 | tf_op jit(solution)/shard_map/ppermute | solution.py:370
  7.9 0.9 %turn.1 = (f32[2048,128]{1,0:T(8,128)S(1)}, f32[32,128]{1,0:T(8,128)S(1)}) custom-call(f32[2048,128]{1,0:T(8,128)S(1)} %get-tuple-element.24.x_ref, s32[4,2,16]{2,1,0:T(2,128)} %cut_hbm.1, s32[4]{0:T(128)} %reach_hbm.1), custom_call_target="tpu_custom_call" | custom-call | flops 10000000 | tf_op jit(solution)/shard_map/turn/pallas_call | solution.py:411
  8.8 0.7 %collective-permute-done.2 = f32[8,128]{1,0:T(8,128)S(1)} collective-permute-done((f32[8,128]{1,0:T(8,128)S(1)}, f32[8,128]{1,0:T(8,128)S(1)}, u32[]{:S(2)}, u32[]{:S(2)}) %collective-permute-start.2) | collective-permute-done | bytes 4128 | tf_op jit(solution)/shard_map/ppermute | solution.py:370
  9.5 0.0 collective-permute-done.3
  9.5 0.0 collective-permute-done.1
  9.5 0.8 %collective-permute-start.4 = (f32[8,128]{1,0:T(8,128)S(1)}, f32[8,128]{1,0:T(8,128)S(1)}, u32[]{:S(2)}, u32[]{:S(2)}) collective-permute-start(f32[8,128]{1,0:T(8,128)S(1)} %get-tuple-element.34.own_ref), channel_id=1, source_target_pairs={{0,1},{1,0},{2,3},{3,2},{4,5},{5,4},{6,7},{7,6},{8,9},{9,8},{10,11... | collective-permute-start | bytes 12296 | tf_op jit(solution)/shard_map/ppermute | solution.py:370
  10.3 0.8 %main.1 = (f32[2176,128]{1,0:T(8,128)S(1)}, f32[1152,128]{1,0:T(8,128)S(1)}, s32[40,128]{1,0:T(8,128)S(1)}, f32[96,128]{1,0:T(8,128)S(1)}) custom-call(f32[64,128]{1,0:T(8,128)S(1)} %get-tuple-element.22.gain_ref, s32[64,128]{1,0:T(8,128)S(1)} %get-tuple-element.23.bins_ref, f32[8,128]{1,0:T(8,128)S(1)} %get-tuple-element.34.own_ref, ...), custom_call_target="tpu_custom_call" | custom-call | flops 10000000 | tf_op jit(solution)/shard_map/main/pallas_call | solution.py:470
  11.1 0.0 collective-permute-done.4
  11.1 0.3 %rim.1 = (f32[1152,128]{1,0:T(8,128)S(1)}, f32[128,128]{1,0:T(8,128)S(1)}) custom-call(f32[8,128]{1,0:T(8,128)S(1)} %broadcast_select_fusion.next_ref, s32[40,128]{1,0:T(8,128)S(1)} %get-tuple-element.27.rim_index_ref, f32[1152,128]{1,0:T(8,128)S(1)} %get-tuple-element.28.half_tail_ref, f32[96,128]{1,0:T(8,128)S(1)} %get-tuple-element.29.head_ref, ...), custom_call_target="tpu_custom_call" | custom-call | tf_op jit(solution)/shard_map/rim/pallas_call | solution.py:486
  11.5 1.7 %collective-permute-start.5 = (f32[128,128]{1,0:T(8,128)S(1)}, f32[128,128]{1,0:T(8,128)S(1)}, u32[]{:S(2)}, u32[]{:S(2)}) collective-permute-start(f32[128,128]{1,0:T(8,128)S(1)} %get-tuple-element.30), channel_id=1, source_target_pairs={{0,16},{1,17},{2,18},{3,19},{4,20},{5,21},{6,22},{7,23},{8,24},{9,... | collective-permute-start | bytes 196616 | tf_op jit(solution)/shard_map/ppermute | solution.py:370
  13.1 1.1 %own.1._ = f32[256,128]{1,0:T(8,128)} custom-call(f32[2176,128]{1,0:T(8,128)S(1)} %get-tuple-element.31.normal_ref, f32[1152,128]{1,0:T(8,128)S(1)} %get-tuple-element.32.tail_ref, f32[32,128]{1,0:T(8,128)S(1)} %get-tuple-element.26.cuts_ref), custom_call_target="tpu_custom_call" | custom-call | flops 10000000 | tf_op jit(solution)/shard_map/own/pallas_call | solution.py:513
  14.2 1.6 %collective-permute-done.5.scores_ref = f32[128,128]{1,0:T(8,128)S(1)} collective-permute-done((f32[128,128]{1,0:T(8,128)S(1)}, f32[128,128]{1,0:T(8,128)S(1)}, u32[]{:S(2)}, u32[]{:S(2)}) %collective-permute-start.5) | collective-permute-done | bytes 65568 | tf_op jit(solution)/shard_map/ppermute | solution.py:370
  15.9 0.6 %place.1 = f32[256,128]{1,0:T(8,128)} custom-call(f32[128,128]{1,0:T(8,128)S(1)} %collective-permute-done.5.scores_ref, f32[256,128]{1,0:T(8,128)} %own.1._), custom_call_target="tpu_custom_call", output_to_operand_aliasing={{}: (1, {})} | custom-call | tf_op jit(solution)/shard_map/place/pallas_call | solution.py:526
  (7 shorter events, 0.0 us)
Async XLA Ops:
  1.5 1.4 %collective-permute-start = (f32[24,128]{1,0:T(8,128)S(1)}, f32[24,128]{1,0:T(8,128)S(1)}, u32[]{:S(2)}, u32[]{:S(2)}) collective-permute-start(f32[24,128]{1,0:T(8,128)S(1)} %get-tuple-element.19), channel_id=1, source_target_pairs={{0,1},{1,0},{2,3},{3,2},{4,5},{5,4},{6,7},{7,6},{8,9},{9,8},{10,11... | collective-permute-start | bytes 36872 | tf_op jit(solution)/shard_map/ppermute | solution.py:370
  2.9 6.5 %collective-permute-start.1 = (f32[16,128]{1,0:T(8,128)S(1)}, f32[16,128]{1,0:T(8,128)S(1)}, u32[]{:S(2)}, u32[]{:S(2)}) collective-permute-start(f32[16,128]{1,0:T(8,128)S(1)} %pad_maximum_fusion), channel_id=1, source_target_pairs={{0,16},{1,2},{2,1},{3,4},{4,3},{5,6},{6,5},{7,8},{8,7},{9,10},{10,... | collective-permute-start | bytes 24584 | tf_op jit(solution)/shard_map/ppermute | solution.py:370
  5.8 3.6 %collective-permute-start.2 = (f32[8,128]{1,0:T(8,128)S(1)}, f32[8,128]{1,0:T(8,128)S(1)}, u32[]{:S(2)}, u32[]{:S(2)}) collective-permute-start(f32[8,128]{1,0:T(8,128)S(1)} %get-tuple-element.21), channel_id=1, source_target_pairs={{0,16},{1,17},{2,18},{3,19},{4,20},{5,21},{6,22},{7,23},{8,24},{9,... | collective-permute-start | bytes 12296 | tf_op jit(solution)/shard_map/ppermute | solution.py:370
  5.9 3.5 %collective-permute-start.3 = (f32[8,128]{1,0:T(8,128)S(1)}, f32[8,128]{1,0:T(8,128)S(1)}, u32[]{:S(2)}, u32[]{:S(2)}) collective-permute-start(f32[8,128]{1,0:T(8,128)S(1)} %get-tuple-element.21), channel_id=1, source_target_pairs={{0,16},{1,18},{2,17},{3,20},{4,19},{5,22},{6,21},{7,24},{8,23},{9,... | collective-permute-start | bytes 12296 | tf_op jit(solution)/shard_map/ppermute | solution.py:370
  9.5 1.6 %collective-permute-start.4 = (f32[8,128]{1,0:T(8,128)S(1)}, f32[8,128]{1,0:T(8,128)S(1)}, u32[]{:S(2)}, u32[]{:S(2)}) collective-permute-start(f32[8,128]{1,0:T(8,128)S(1)} %get-tuple-element.34.own_ref), channel_id=1, source_target_pairs={{0,1},{1,0},{2,3},{3,2},{4,5},{5,4},{6,7},{7,6},{8,9},{9,8},{10,11... | collective-permute-start | bytes 12296 | tf_op jit(solution)/shard_map/ppermute | solution.py:370
  11.5 4.4 %collective-permute-start.5 = (f32[128,128]{1,0:T(8,128)S(1)}, f32[128,128]{1,0:T(8,128)S(1)}, u32[]{:S(2)}, u32[]{:S(2)}) collective-permute-start(f32[128,128]{1,0:T(8,128)S(1)} %get-tuple-element.30), channel_id=1, source_target_pairs={{0,16},{1,17},{2,18},{3,19},{4,20},{5,21},{6,22},{7,23},{8,24},{9,... | collective-permute-start | bytes 196616 | tf_op jit(solution)/shard_map/ppermute | solution.py:370
where the time goes:
time: 16.7 us; the launch traced here: 16.5 us
  starting transfers between devices  7.98 us (48%)
  Pallas kernels  5.28 us (32%)
  waiting for transfers between devices  3.14 us (19%)
    ppermute x6, starting transfers between devices, swap(): return lax.ppermute(value, BOTH, route)  7.98 us
    ppermute x6, waiting for transfers between devices, swap(): return lax.ppermute(value, BOTH, route)  3.14 us
    pallas_call x1, Pallas kernels, search(): pl.pallas_call(functools.partial(bin_kernel, groups, integrations, bin_ti...  1.52 us
    pallas_call x1, Pallas kernels, search(): pl.pallas_call(functools.partial(own_kernel, sizes), out_shape=out_shape,...  1.1 us
    pallas_call x1, Pallas kernels, search(): pl.pallas_call(functools.partial(turn_kernel, groups, integrations), out_...  0.9 us
    pallas_call x1, Pallas kernels, search(): pl.pallas_call(functools.partial(main_kernel, sizes), out_shape=(shape((i...  0.8 us
    pallas_call x1, Pallas kernels, search(): pl.pallas_call(functools.partial(place_kernel, hop), out_shape=out_shape,...  0.64 us
  transfers between devices with their start and end apart: 6, of which 3 were waited for; matrix products, arithmetic and copies ran while one was open for 0% of the time, Pallas kernels for 17%

commit v1 on v0

--- a/solution.py
+++ b/solution.py
@@ -254,16 +254,18 @@
 
 
 def rim_kernel(
-    sizes, next_ref, rim_index_ref, half_tail_ref, head_ref, cuts_ref, tail_ref, out_ref, *later_refs
+    sizes, own_ref, mate_ref, rim_index_ref, half_tail_ref, head_ref, cuts_ref, tail_ref, out_ref, *later_refs
 ):
     groups, integrations = sizes.groups, sizes.integrations
     cols = LANES // groups
     lane = lane_iota()
     at_end = lax.axis_index("freq") == lax.axis_size("freq") - 1
     last_col = lane % cols == cols - 1
-    inverse = inverse_levels(groups, integrations, sizes.bin_tiles, next_ref)
+    odd = lax.rem(lax.axis_index("freq"), 2) == 1
+    table = jnp.where(odd, own_ref[...], mate_ref[...])
+    inverse = inverse_levels(groups, integrations, sizes.bin_tiles, table)
     inner = LANES - sizes.head
-    for row in range(0, sizes.extra, SUBS):
+    for row in range(0, sizes.extra - SUBS, SUBS):
         index = rim_index_ref[row : row + SUBS, :]
         level = look_up(inverse[0], index)
         for group in range(1, groups):
@@ -273,9 +275,6 @@
             half = half_tail_ref[at : at + SUBS, :]
             edge = jnp.where(at_end, 0.0, half * level - 1.0)
             tail_ref[at : at + SUBS, :] = jnp.where(last_col, edge, half)
-    for t in range(integrations):
-        at = t * sizes.tail_span
-        tail_ref[at : at + inner, :] = half_tail_ref[at : at + inner, :]
     for index in range(sizes.strides):
         head = head_ref[index * sizes.head : (index + 1) * sizes.head, :]
         rest = tree(sizes, 1, index, tail_ref, sizes.tail_span, LANES - sizes.head, cuts_ref, later_refs)
@@ -456,7 +455,7 @@
         earlier_across = swap(earlier, across)
         own = own + earlier + jnp.where(has_across, earlier_across, 0.0)
     odd = freq % 2 == 1
-    following = jnp.where(odd, own, swap(own, mate))
+    mate_table = swap(own, mate)
     next_rim = jnp.where(odd, from_across[rows:], from_mate[2 * rows :])
     next_bins = jnp.where(odd, from_across[SUBS - 2 : SUBS - 1], from_mate[SUBS - 1 : SUBS])
 
@@ -486,12 +485,13 @@
     tail, first_scores = pl.pallas_call(
         functools.partial(rim_kernel, sizes),
         out_shape=(shape(half_tail.shape), scores_shape),
-        in_specs=[VMEM] * 5,
+        in_specs=[VMEM] * 6,
+        input_output_aliases={3: 0},
         out_specs=(VMEM, VMEM),
         scratch_shapes=later(sizes.tail_span),
         compiler_params=PARAMS,
         name="rim",
-    )(following, rim_index, half_tail, head, cuts)
+    )(own, mate_table, rim_index, half_tail, head, cuts)
 
     def scores(hop):
         return pl.pallas_call(

time: 16.7 us -> 16.7 us (level)
  no operation moved by 1% of the time
where the time goes in v1:
time: 16.7 us; the launch traced here: 16.5 us
  starting transfers between devices  7.95 us (48%)
  Pallas kernels  5.35 us (32%)
  waiting for transfers between devices  3.11 us (19%)
    ppermute x6, starting transfers between devices, swap(): return lax.ppermute(value, BOTH, route)  7.95 us
    ppermute x6, waiting for transfers between devices, swap(): return lax.ppermute(value, BOTH, route)  3.11 us
    pallas_call x1, Pallas kernels, search(): pl.pallas_call(functools.partial(bin_kernel, groups, integrations, bin_ti...  1.52 us
    pallas_call x1, Pallas kernels, search(): pl.pallas_call(functools.partial(own_kernel, sizes), out_shape=out_shape,...  1.12 us
    pallas_call x1, Pallas kernels, search(): pl.pallas_call(functools.partial(turn_kernel, groups, integrations), out_...  0.9 us
    pallas_call x1, Pallas kernels, search(): pl.pallas_call(functools.partial(main_kernel, sizes), out_shape=(shape((i...  0.82 us
    pallas_call x1, Pallas kernels, search(): pl.pallas_call(functools.partial(place_kernel, hop), out_shape=out_shape,...  0.64 us
    pallas_call x1, Pallas kernels, search(): pl.pallas_call(functools.partial(rim_kernel, sizes), out_shape=(shape(hal...  0.35 us
  transfers between devices with their start and end apart: 6, of which 3 were waited for; matrix products, arithmetic and copies ran while one was open for 0% of the time, Pallas kernels for 17%

profile of v1, /device:TPU:0, one launch (start us, length us, event | category | flops | bytes accessed | tf_op | source)
XLA Modules:
  0.0 16.5 jit_solution(13221261055130740080)
XLA Ops:
  0.0 1.5 %bin_sums.1 = (f32[24,128]{1,0:T(8,128)S(1)}, f32[2048,128]{1,0:T(8,128)S(1)}, f32[64,128]{1,0:T(8,128)S(1)}, s32[64,128]{1,0:T(8,128)S(1)}) custom-call(f32[2048,128]{1,0:T(8,128)} %bitcast.8, f32[64,128]{1,0:T(8,128)} %bitcast.9, s32[64,128]{1,0:T(8,128)} %bitcast.10), custom_call_target="tpu_custom_call" | custom-call | tf_op jit(solution)/shard_map/bin_sums/pallas_call | solution.py:395
  1.5 0.6 %collective-permute-start = (f32[24,128]{1,0:T(8,128)S(1)}, f32[24,128]{1,0:T(8,128)S(1)}, u32[]{:S(2)}, u32[]{:S(2)}) collective-permute-start(f32[24,128]{1,0:T(8,128)S(1)} %get-tuple-element.19), channel_id=1, source_target_pairs={{0,1},{1,0},{2,3},{3,2},{4,5},{5,4},{6,7},{7,6},{8,9},{9,8},{10,11... | collective-permute-start | bytes 36872 | tf_op jit(solution)/shard_map/ppermute | solution.py:369
  2.1 0.8 %collective-permute-done = f32[24,128]{1,0:T(8,128)S(1)} collective-permute-done((f32[24,128]{1,0:T(8,128)S(1)}, f32[24,128]{1,0:T(8,128)S(1)}, u32[]{:S(2)}, u32[]{:S(2)}) %collective-permute-start) | collective-permute-done | bytes 12320 | tf_op jit(solution)/shard_map/ppermute | solution.py:369
  2.9 2.9 %collective-permute-start.1 = (f32[16,128]{1,0:T(8,128)S(1)}, f32[16,128]{1,0:T(8,128)S(1)}, u32[]{:S(2)}, u32[]{:S(2)}) collective-permute-start(f32[16,128]{1,0:T(8,128)S(1)} %pad_maximum_fusion), channel_id=1, source_target_pairs={{0,16},{1,2},{2,1},{3,4},{4,3},{5,6},{6,5},{7,8},{8,7},{9,10},{10,... | collective-permute-start | bytes 24584 | tf_op jit(solution)/shard_map/ppermute | solution.py:369
  5.8 0.1 collective-permute-start.2
  5.9 1.9 %collective-permute-start.3 = (f32[8,128]{1,0:T(8,128)S(1)}, f32[8,128]{1,0:T(8,128)S(1)}, u32[]{:S(2)}, u32[]{:S(2)}) collective-permute-start(f32[8,128]{1,0:T(8,128)S(1)} %get-tuple-element.21), channel_id=1, source_target_pairs={{0,16},{1,18},{2,17},{3,20},{4,19},{5,22},{6,21},{7,24},{8,23},{9,... | collective-permute-start | bytes 12296 | tf_op jit(solution)/shard_map/ppermute | solution.py:369
  7.9 0.9 %turn.1 = (f32[2048,128]{1,0:T(8,128)S(1)}, f32[32,128]{1,0:T(8,128)S(1)}) custom-call(f32[2048,128]{1,0:T(8,128)S(1)} %get-tuple-element.24.x_ref, s32[4,2,16]{2,1,0:T(2,128)} %cut_hbm.1, s32[4]{0:T(128)} %reach_hbm.1), custom_call_target="tpu_custom_call" | custom-call | flops 10000000 | tf_op jit(solution)/shard_map/turn/pallas_call | solution.py:410
  8.8 0.7 %collective-permute-done.2 = f32[8,128]{1,0:T(8,128)S(1)} collective-permute-done((f32[8,128]{1,0:T(8,128)S(1)}, f32[8,128]{1,0:T(8,128)S(1)}, u32[]{:S(2)}, u32[]{:S(2)}) %collective-permute-start.2) | collective-permute-done | bytes 4128 | tf_op jit(solution)/shard_map/ppermute | solution.py:369
  9.5 0.0 collective-permute-done.3
  9.5 0.0 collective-permute-done.1
  9.5 0.8 %collective-permute-start.4 = (f32[8,128]{1,0:T(8,128)S(1)}, f32[8,128]{1,0:T(8,128)S(1)}, u32[]{:S(2)}, u32[]{:S(2)}) collective-permute-start(f32[8,128]{1,0:T(8,128)S(1)} %get-tuple-element.34.own_ref), channel_id=1, source_target_pairs={{0,1},{1,0},{2,3},{3,2},{4,5},{5,4},{6,7},{7,6},{8,9},{9,8},{10,11... | collective-permute-start | bytes 12296 | tf_op jit(solution)/shard_map/ppermute | solution.py:369
  10.3 0.8 %main.1 = (f32[2176,128]{1,0:T(8,128)S(1)}, f32[1152,128]{1,0:T(8,128)S(1)}, s32[40,128]{1,0:T(8,128)S(1)}, f32[96,128]{1,0:T(8,128)S(1)}) custom-call(f32[64,128]{1,0:T(8,128)S(1)} %get-tuple-element.22.gain_ref, s32[64,128]{1,0:T(8,128)S(1)} %get-tuple-element.23.bins_ref, f32[8,128]{1,0:T(8,128)S(1)} %get-tuple-element.34.own_ref, ...), custom_call_target="tpu_custom_call" | custom-call | flops 10000000 | tf_op jit(solution)/shard_map/main/pallas_call | solution.py:469
  11.1 0.0 collective-permute-done.4.mate_ref
  11.1 0.3 %rim.1 = (f32[1152,128]{1,0:T(8,128)S(1)}, f32[128,128]{1,0:T(8,128)S(1)}) custom-call(f32[8,128]{1,0:T(8,128)S(1)} %get-tuple-element.34.own_ref, f32[8,128]{1,0:T(8,128)S(1)} %collective-permute-done.4.mate_ref, s32[40,128]{1,0:T(8,128)S(1)} %get-tuple-element.27.rim_index_ref, ...), custom_call_target="tpu_custom_call", output_to_operand_aliasing={{0}: (3, {})} | custom-call | tf_op jit(solution)/shard_map/rim/pallas_call | solution.py:485
  11.5 1.7 %collective-permute-start.5 = (f32[128,128]{1,0:T(8,128)S(1)}, f32[128,128]{1,0:T(8,128)S(1)}, u32[]{:S(2)}, u32[]{:S(2)}) collective-permute-start(f32[128,128]{1,0:T(8,128)S(1)} %get-tuple-element.30), channel_id=1, source_target_pairs={{0,16},{1,17},{2,18},{3,19},{4,20},{5,21},{6,22},{7,23},{8,24},{9,... | collective-permute-start | bytes 196616 | tf_op jit(solution)/shard_map/ppermute | solution.py:369
  13.1 1.1 %own.1._ = f32[256,128]{1,0:T(8,128)} custom-call(f32[2176,128]{1,0:T(8,128)S(1)} %get-tuple-element.31.normal_ref, f32[1152,128]{1,0:T(8,128)S(1)} %get-tuple-element.32.tail_ref, f32[32,128]{1,0:T(8,128)S(1)} %get-tuple-element.26.cuts_ref), custom_call_target="tpu_custom_call" | custom-call | flops 10000000 | tf_op jit(solution)/shard_map/own/pallas_call | solution.py:513
  14.3 1.6 %collective-permute-done.5.scores_ref = f32[128,128]{1,0:T(8,128)S(1)} collective-permute-done((f32[128,128]{1,0:T(8,128)S(1)}, f32[128,128]{1,0:T(8,128)S(1)}, u32[]{:S(2)}, u32[]{:S(2)}) %collective-permute-start.5) | collective-permute-done | bytes 65568 | tf_op jit(solution)/shard_map/ppermute | solution.py:369
  15.9 0.6 %place.1 = f32[256,128]{1,0:T(8,128)} custom-call(f32[128,128]{1,0:T(8,128)S(1)} %collective-permute-done.5.scores_ref, f32[256,128]{1,0:T(8,128)} %own.1._), custom_call_target="tpu_custom_call", output_to_operand_aliasing={{}: (1, {})} | custom-call | tf_op jit(solution)/shard_map/place/pallas_call | solution.py:526
  (6 shorter events, 0.0 us)
Async XLA Ops:
  1.5 1.4 %collective-permute-start = (f32[24,128]{1,0:T(8,128)S(1)}, f32[24,128]{1,0:T(8,128)S(1)}, u32[]{:S(2)}, u32[]{:S(2)}) collective-permute-start(f32[24,128]{1,0:T(8,128)S(1)} %get-tuple-element.19), channel_id=1, source_target_pairs={{0,1},{1,0},{2,3},{3,2},{4,5},{5,4},{6,7},{7,6},{8,9},{9,8},{10,11... | collective-permute-start | bytes 36872 | tf_op jit(solution)/shard_map/ppermute | solution.py:369
  2.9 6.5 %collective-permute-start.1 = (f32[16,128]{1,0:T(8,128)S(1)}, f32[16,128]{1,0:T(8,128)S(1)}, u32[]{:S(2)}, u32[]{:S(2)}) collective-permute-start(f32[16,128]{1,0:T(8,128)S(1)} %pad_maximum_fusion), channel_id=1, source_target_pairs={{0,16},{1,2},{2,1},{3,4},{4,3},{5,6},{6,5},{7,8},{8,7},{9,10},{10,... | collective-permute-start | bytes 24584 | tf_op jit(solution)/shard_map/ppermute | solution.py:369
  5.8 3.6 %collective-permute-start.2 = (f32[8,128]{1,0:T(8,128)S(1)}, f32[8,128]{1,0:T(8,128)S(1)}, u32[]{:S(2)}, u32[]{:S(2)}) collective-permute-start(f32[8,128]{1,0:T(8,128)S(1)} %get-tuple-element.21), channel_id=1, source_target_pairs={{0,16},{1,17},{2,18},{3,19},{4,20},{5,21},{6,22},{7,23},{8,24},{9,... | collective-permute-start | bytes 12296 | tf_op jit(solution)/shard_map/ppermute | solution.py:369
  5.9 3.5 %collective-permute-start.3 = (f32[8,128]{1,0:T(8,128)S(1)}, f32[8,128]{1,0:T(8,128)S(1)}, u32[]{:S(2)}, u32[]{:S(2)}) collective-permute-start(f32[8,128]{1,0:T(8,128)S(1)} %get-tuple-element.21), channel_id=1, source_target_pairs={{0,16},{1,18},{2,17},{3,20},{4,19},{5,22},{6,21},{7,24},{8,23},{9,... | collective-permute-start | bytes 12296 | tf_op jit(solution)/shard_map/ppermute | solution.py:369
  9.5 1.6 %collective-permute-start.4 = (f32[8,128]{1,0:T(8,128)S(1)}, f32[8,128]{1,0:T(8,128)S(1)}, u32[]{:S(2)}, u32[]{:S(2)}) collective-permute-start(f32[8,128]{1,0:T(8,128)S(1)} %get-tuple-element.34.own_ref), channel_id=1, source_target_pairs={{0,1},{1,0},{2,3},{3,2},{4,5},{5,4},{6,7},{7,6},{8,9},{9,8},{10,11... | collective-permute-start | bytes 12296 | tf_op jit(solution)/shard_map/ppermute | solution.py:369
  11.5 4.4 %collective-permute-start.5 = (f32[128,128]{1,0:T(8,128)S(1)}, f32[128,128]{1,0:T(8,128)S(1)}, u32[]{:S(2)}, u32[]{:S(2)}) collective-permute-start(f32[128,128]{1,0:T(8,128)S(1)} %get-tuple-element.30), channel_id=1, source_target_pairs={{0,16},{1,17},{2,18},{3,19},{4,20},{5,21},{6,22},{7,23},{8,24},{9,... | collective-permute-start | bytes 196616 | tf_op jit(solution)/shard_map/ppermute | solution.py:369
